TPU v7x, 256 devices: a whole 4x4x8 slice. The times are simulated.
256 devices in a mesh: row: 32 (over x, z_lo, core), chan: 8 (over y, z_hi).
Axes of the slice: x: 4, y: 4, z: 8 (z_hi: 2, z_lo: 4; z = z_hi * 4 + z_lo), core: 2. Of those that a mesh axis runs over, the one named last changes fastest.
Arguments:
- pair: bfloat16 [128, 768, 768], P('chan', 'row'), may hold values from -24 to 24
- single: bfloat16 [768, 384], P('row'), may hold values from -6 to 6
- token_mask: int32 [768], replicated, may hold values from 0 to 1, as said below
- pair_gain: float32 [128], replicated, may hold values from 0.5 to 1.5
- w_ab: bfloat16 [128, 4, 128], replicated, may hold values from -0.5 to 0.5
- w_out_gate: bfloat16 [128, 128], replicated, may hold values from -0.5 to 0.5
- x_gain: float32 [128], replicated, may hold values from 0.5 to 1.5
- w_tri_out: bfloat16 [128, 128], replicated, may hold values from -0.5 to 0.5
- bias_gain: float32 [128], replicated, may hold values from 0.5 to 1.5
- w_bias: bfloat16 [128, 16], replicated, may hold values from -0.5 to 0.5
- single_gain: float32 [384], replicated, may hold values from 0.5 to 1.5
- w_query: bfloat16 [384, 384], P(None, 'chan'), may hold values from -1 to 1
- w_key: bfloat16 [384, 384], P(None, 'chan'), may hold values from -16 to 16
- w_value_gate: bfloat16 [384, 2, 384], P(None, None, 'chan'), may hold values from -0.3125 to 0.3125
- w_mix: bfloat16 [384, 384], P('chan'), may hold values from -0.3125 to 0.3125
Outputs:
- pair_out: bfloat16 [128, 768, 768], P('chan', 'row')
- attended: bfloat16 [768, 384], P('row', 'chan')
Inputs may be any that keep to these rules, and one draw needn't show every extreme that they name: token_mask is 1 on the first tokens and 0 on the rest; at least 672 tokens are real.
All inputs are finite; a program needn't handle non-finite values.
Results may differ from a plain program's by a relative error of at most 0.015.
The roundings to bfloat16 on the way count: a program that leaves them out, or rounds other values in their place, can miss the bound.
Values may be sent and summed in bfloat16 or wider, within the bound.
No kernel may reach another device: no remote copies, remote signals or barrier semaphores. Data moves between devices by JAX's collectives and lax.ppermute only.
A program may use at most 64 MiB of HBM per device.

v0:
```python
import jax
import jax.numpy as jnp
from jax import lax
from jax.sharding import Mesh
from jax.sharding import PartitionSpec as P

D = 384
H = 16
CHAN = ("chan_0", "chan_1")
EPS = 1e-05


def gathered_by_axis(shard, axes, dim):
    for axis in reversed(axes):
        shard = lax.all_gather(shard, axis, axis=dim, tiled=True)
    return shard


def sent_together(arrays, axis, dim, along):
    widths = [a.shape[along] for a in arrays]
    both = jnp.concatenate(arrays, axis=along)
    whole = lax.all_gather(both, axis, axis=dim, tiled=True)
    return tuple(jnp.split(whole, [sum(widths[:k]) for k in range(1, len(widths))], axis=along))


def cut_along(shard, dim, peers):
    before, after = (shard.shape[:dim], shard.shape[dim + 1 :])
    return jnp.moveaxis(shard.reshape(*before, peers, -1, *after), dim, 0)


def sent_and_summed(shard, axis, dim):
    peers = lax.axis_size(axis)
    blocks = lax.all_to_all(cut_along(shard, dim, peers), axis, 0, 0, tiled=True)
    return jnp.sum(blocks.astype(jnp.float32), axis=0)


def layer_norm(values, gain, axis):
    middle = jnp.mean(values, axis=axis, keepdims=True)
    centred = values - middle
    spread = jnp.mean(centred * centred, axis=axis, keepdims=True)
    return centred * lax.rsqrt(spread + EPS) * gain


def body(
    pair,
    single,
    token_mask,
    pair_gain,
    w_ab,
    w_out_gate,
    x_gain,
    w_tri_out,
    bias_gain,
    w_bias,
    single_gain,
    w_query,
    w_key,
    w_value_gate,
    w_mix,
):
    chans = pair.shape[0]
    rows = pair.shape[1]
    width = pair.shape[2]
    ranks = lax.axis_size("row")
    chan_start = lax.axis_index(CHAN) * chans
    row_start = lax.axis_index("row") * rows
    live = token_mask.astype(jnp.float32)
    live_rows = lax.dynamic_slice_in_dim(live, row_start, rows, 0)
    pair_mask = live_rows[:, None] * live[None, :]
    full = gathered_by_axis(pair, CHAN, 0)
    normed = layer_norm(full.astype(jnp.float32), pair_gain[:, None, None], 0).astype(jnp.bfloat16)
    w_own = lax.dynamic_slice_in_dim(w_ab, chan_start, chans, 2)
    share = max(1, ranks // chans)
    per_owner = max(1, chans // ranks)
    groups = chans // per_owner
    part_rows = rows // share
    projected = jnp.einsum("cik,cpd->pdik", normed, w_own, preferred_element_type=jnp.float32)
    left = (jax.nn.sigmoid(projected[0]) * projected[1] * pair_mask[None]).astype(jnp.bfloat16)
    right = (jax.nn.sigmoid(projected[2]) * projected[3] * pair_mask[None]).astype(jnp.bfloat16)
    left_send = left.reshape(groups, per_owner, share, part_rows, width).transpose(0, 2, 1, 3, 4)
    left_send = left_send.reshape(ranks * per_owner, part_rows, width)
    right_send = jnp.broadcast_to(
        right.reshape(groups, 1, per_owner, rows, width), (groups, share, per_owner, rows, width)
    )
    right_send = right_send.reshape(ranks * per_owner, rows, width)
    left_owned, right_owned = (
        lax.all_to_all(left_send, "row", split_axis=0, concat_axis=1, tiled=True),
        lax.all_to_all(right_send, "row", split_axis=0, concat_axis=1, tiled=True),
    )
    owned = jnp.einsum(
        "uik,ujk->uij", left_owned, right_owned, preferred_element_type=jnp.float32
    ).astype(jnp.bfloat16)
    returned = lax.all_to_all(owned, "row", split_axis=1, concat_axis=0, tiled=True)
    summed = (
        returned.reshape(groups, share, per_owner, part_rows, width)
        .transpose(0, 2, 1, 3, 4)
        .reshape(chans, rows, width)
    )
    crossed = lax.all_gather(summed, CHAN, axis=0, tiled=True)
    product_normed = layer_norm(crossed.astype(jnp.float32), x_gain[:, None, None], 0).astype(
        jnp.bfloat16
    )
    out_gate = jax.nn.sigmoid(
        jnp.einsum("cij,cd->dij", normed, w_out_gate, preferred_element_type=jnp.float32)
    )
    update = jnp.einsum(
        "cij,cd->dij", product_normed, w_tri_out, preferred_element_type=jnp.float32
    )
    renewed = (full.astype(jnp.float32) + out_gate * update).astype(jnp.bfloat16)
    pair_out = lax.dynamic_slice_in_dim(renewed, chan_start, chans, 0)
    head_size = D // H
    local_width = w_query.shape[1]
    heads = local_width // head_size
    head_start = lax.axis_index(CHAN) * heads
    bias_input = layer_norm(renewed.astype(jnp.float32), bias_gain[:, None, None], 0).astype(
        jnp.bfloat16
    )
    w_bias_own = lax.dynamic_slice_in_dim(w_bias, head_start, heads, 1)
    bias = jnp.einsum("cij,ch->hij", bias_input, w_bias_own, preferred_element_type=jnp.float32)
    single_normed = layer_norm(single.astype(jnp.float32), single_gain[None, :], 1).astype(
        jnp.bfloat16
    )
    queries = jnp.dot(single_normed, w_query, preferred_element_type=jnp.float32).astype(
        jnp.bfloat16
    )
    head_gate = jax.nn.sigmoid(
        jnp.dot(single_normed, w_value_gate[:, 1, :], preferred_element_type=jnp.float32)
    )
    own_keys = jnp.dot(single_normed, w_key, preferred_element_type=jnp.float32).astype(
        jnp.bfloat16
    )
    own_values = jnp.dot(
        single_normed, w_value_gate[:, 0, :], preferred_element_type=jnp.float32
    ).astype(jnp.bfloat16)
    keys, values = sent_together((own_keys, own_values), "row", 0, 1)
    tokens = keys.shape[0]
    query_heads = queries.reshape(rows, heads, head_size)
    key_heads = keys.reshape(tokens, heads, head_size)
    value_heads = values.reshape(tokens, heads, head_size)
    scores = jnp.einsum("ihe,jhe->hij", query_heads, key_heads, preferred_element_type=jnp.float32)
    scores = scores / jnp.sqrt(jnp.float32(head_size)) + bias
    scores = jnp.where(live[None, None, :] > 0, scores, -jnp.inf)
    top = jnp.max(scores, axis=2, keepdims=True)
    raised = jnp.exp(scores - top)
    weights = (raised / jnp.sum(raised, axis=2, keepdims=True)).astype(jnp.bfloat16)
    mixed = jnp.einsum("hij,jhe->ihe", weights, value_heads, preferred_element_type=jnp.float32)
    heads_out = (mixed.reshape(rows, local_width) * head_gate).astype(jnp.bfloat16)
    terms = jnp.dot(heads_out, w_mix, preferred_element_type=jnp.float32)
    attended = sent_and_summed(terms.astype(jnp.bfloat16), CHAN, 1).astype(jnp.bfloat16)
    return (pair_out, attended)


def solution(mesh):
    split = Mesh(mesh.devices.reshape(mesh.shape["row"], 4, 2), ("row", "chan_0", "chan_1"))
    return jax.shard_map(
        body,
        mesh=split,
        in_specs=(
            P(CHAN, "row", None),
            P("row", None),
            P(),
            P(),
            P(),
            P(),
            P(),
            P(),
            P(),
            P(),
            P(),
            P(None, CHAN),
            P(None, CHAN),
            P(None, None, CHAN),
            P(CHAN, None),
        ),
        out_specs=(P(CHAN, "row", None), P("row", CHAN)),
        check_vma=False,
    )
```

profile of v0, /device:TPU:2, one launch (start us, length us, event | category | flops | bytes accessed | tf_op | source)
XLA Modules:
  0.0 371.6 jit_solution(35078988886564830)
XLA Ops:
  7.2 2.0 copy.73
  9.3 48.9 %all-gather.4.cloned.1.call-done = bf16[32,24,768]{2,0,1:T(8,128)(2,1)} async-done(((bf16[16,24,768]{2,0,1:T(8,128)(2,1)}), bf16[32,24,768]{2,0,1:T(8,128)(2,1)}) %all-gather.4.cloned.1.call-update) | async-done | bytes 1179664 | tf_op jit(solution)/shard_map/all_gather | solution.py:15
  59.6 51.7 %all-gather.6.cloned.1.call-done = bf16[128,24,768]{2,0,1:T(8,128)(2,1)} async-done(((bf16[32,24,768]{2,0,1:T(8,128)(2,1)}), bf16[128,24,768]{2,0,1:T(8,128)(2,1)}) %all-gather.6.cloned.1.call-update) | async-done | bytes 4718608 | tf_op jit(solution)/shard_map/all_gather | solution.py:15
  111.3 3.2 convert_reduce_fusion
  116.4 1.9 fusion.17
  118.4 2.2 copy-done.3
  120.9 1.7 copy.76
  122.6 1.4 reshape.164
  125.0 7.9 %all-to-all-start = ((bf16[32,12,768]{2,1,0:T(8,128)(2,1)}), bf16[32,12,768]{2,1,0:T(8,128)(2,1)S(1)}, u32[]{:S(2)}, u32[]{:S(2)}) async-start(bf16[32,12,768]{2,1,0:T(8,128)(2,1)} %multiply_convert_fusion), calls=%async_computation | async-start | bytes 1572864 | tf_op jit(solution)/shard_map/all_to_all | solution.py:87
  132.9 2.0 fusion.26
  135.1 17.5 %all-to-all-done = bf16[32,12,768]{2,1,0:T(8,128)(2,1)S(1)} async-done(((bf16[32,12,768]{2,1,0:T(8,128)(2,1)}), bf16[32,12,768]{2,1,0:T(8,128)(2,1)S(1)}, u32[]{:S(2)}, u32[]{:S(2)}) %all-to-all-start) | async-done | bytes 589856 | tf_op jit(solution)/shard_map/all_to_all | solution.py:87
  153.8 6.4 %all-to-all-start.1 = ((bf16[32,24,768]{2,1,0:T(8,128)(2,1)}), bf16[32,24,768]{2,1,0:T(8,128)(2,1)S(1)}, u32[]{:S(2)}, u32[]{:S(2)}) async-start(bf16[32,24,768]{2,1,0:T(8,128)(2,1)} %bitcast.5), calls=%async_computation.1 | async-start | bytes 2359296 | tf_op jit(solution)/shard_map/all_to_all | solution.py:88
  160.5 27.7 %all-to-all-done.1 = bf16[32,24,768]{2,1,0:T(8,128)(2,1)S(1)} async-done(((bf16[32,24,768]{2,1,0:T(8,128)(2,1)}), bf16[32,24,768]{2,1,0:T(8,128)(2,1)S(1)}, u32[]{:S(2)}, u32[]{:S(2)}) %all-to-all-start.1) | async-done | bytes 1179680 | tf_op jit(solution)/shard_map/all_to_all | solution.py:88
  190.4 4.2 %reduce.1 = bf16[384,768]{1,0:T(8,128)(2,1)S(1)} reduce(bf16[384,1,768]{2,1,0:T(2,128)(2,1)S(1)} %bitcast.64, bf16[]{:T(256)} %broadcast.172), dimensions={1}, to_apply=%bitcast.61.reduce_sub_computation | reduce | bytes 1179650
  194.9 21.7 %all_to_all.32 = bf16[32,2,4608]{2,1,0:T(2,128)(2,1)S(1)} all-to-all(bf16[32,2,4608]{2,1,0:T(2,128)(2,1)S(1)} %reshape.171), channel_id=1, replica_groups=mesh['row'=32,'chan_0'=4,'chan_1'=2] {'row'}, dimensions={0} | all-to-all | bytes 1179648 | tf_op jit(solution)/shard_map/all_to_all | solution.py:93
  218.9 38.8 %all_gather.15 = bf16[768,96]{1,0:T(8,128)(2,1)S(1)} all-gather(bf16[24,96]{1,0:T(8,128)(2,1)S(1)} %pad_maximum_fusion), channel_id=1, replica_groups=mesh['row'=32,'chan_0'=4,'chan_1'=2] {'row'}, dimensions={0}, use_global_device_ids=true | all-gather | bytes 152064 | tf_op jit(solution)/shard_map/all_gather | solution.py:22
  258.4 73.8 %all-gather.8.cloned.1.call-done = bf16[128,24,768]{2,1,0:T(8,128)(2,1)} async-done(((bf16[16,24,768]{2,1,0:T(8,128)(2,1)}), bf16[128,24,768]{2,1,0:T(8,128)(2,1)}) %all-gather.8.cloned.1.call-update) | async-done | bytes 4718608 | tf_op jit(solution)/shard_map/all_gather | solution.py:99
  332.2 3.2 convert_reduce_fusion.2
  337.2 1.4 fusion.15
  338.7 1.4 fusion.19
  340.2 5.2 %convert_reduce_fusion.1 = (f32[24,768]{1,0:T(8,128)S(1)}, bf16[128,24,768]{2,0,1:T(8,128)(2,1)S(1)}) fusion(f32[24,768,128]{1,2,0:T(8,128)S(1)} %fusion.19, bf16[128,128]{1,0:T(8,128)(2,1)S(1)} %copy-done.14, bf16[128,24,768]{2,0,1:T(8,128)(2,1)S(1)} %bitcast.63, f32[128]{0:T(128)S(1)} %copy-done.9, f32[24,768]{1,0:T(8,128)S(1)} %add_rsqrt_fusion.2, ...), kind=kOutput, calls=%fused_computation.5 | convolution fusion | flops 636991488 | bytes 19128832 | tf_op jit(solution)/shard_map/cij,cd->dij/dot_general | solution.py:104
  346.9 2.3 fusion.21
  351.0 3.3 all-to-all-start.3
  356.4 7.9 %all-to-all-done.3 = bf16[8,2,576]{2,1,0:T(2,128)(2,1)S(1)} async-done(((bf16[8,2,576]{2,1,0:T(2,128)(2,1)}), bf16[8,2,576]{2,1,0:T(2,128)(2,1)S(1)}, u32[]{:S(2)}, u32[]{:S(2)}) %all-to-all-start.3) | async-done | bytes 18464 | tf_op jit(solution)/shard_map/all_to_all | solution.py:33
  (96 shorter events, 19.5 us)
Async XLA Ops:
  7.2 51.1 %copy-start = (bf16[128,4,128]{2,1,0:T(4,128)(2,1)S(1)}, bf16[128,4,128]{2,1,0:T(4,128)(2,1)}, u32[]{:S(2)}) copy-start(bf16[128,4,128]{2,1,0:T(4,128)(2,1)} %param.19) | copy-start | bytes 393220
  7.2 51.0 %all-gather.4.cloned.1.call-start = ((), (), s32[]{:S(2)}) async-start(), calls=%async_computation.4 | async-start | bytes 1769472 | tf_op jit(solution)/shard_map/all_gather | solution.py:15
  9.3 102.0 %all-gather.6.cloned.1.call-start = ((), (), s32[]{:S(2)}) async-start(), calls=%async_computation.5 | async-start | bytes 5898240 | tf_op jit(solution)/shard_map/all_gather | solution.py:15
  59.5 56.9 %copy-start.9 = (f32[128]{0:T(128)S(1)}, f32[128]{0:T(128)}, u32[]{:S(2)}) copy-start(f32[128]{0:T(128)} %param.18) | copy-start | bytes 1540
  111.3 3.8 %copy-start.1 = (bf16[128,24,768]{2,0,1:T(8,128)(2,1)S(1)}, bf16[128,24,768]{2,0,1:T(8,128)(2,1)}, u32[]{:S(2)}) copy-start(bf16[128,24,768]{2,0,1:T(8,128)(2,1)} %all-gather.6.cloned.1.call-done) | copy-start | bytes 14155780
  118.4 2.2 copy-start.3
  125.0 27.6 %all-to-all-start = ((bf16[32,12,768]{2,1,0:T(8,128)(2,1)}), bf16[32,12,768]{2,1,0:T(8,128)(2,1)S(1)}, u32[]{:S(2)}, u32[]{:S(2)}) async-start(bf16[32,12,768]{2,1,0:T(8,128)(2,1)} %multiply_convert_fusion), calls=%async_computation | async-start | bytes 1572864 | tf_op jit(solution)/shard_map/all_to_all | solution.py:87
  153.8 34.5 %all-to-all-start.1 = ((bf16[32,24,768]{2,1,0:T(8,128)(2,1)}), bf16[32,24,768]{2,1,0:T(8,128)(2,1)S(1)}, u32[]{:S(2)}, u32[]{:S(2)}) async-start(bf16[32,24,768]{2,1,0:T(8,128)(2,1)} %bitcast.5), calls=%async_computation.1 | async-start | bytes 2359296 | tf_op jit(solution)/shard_map/all_to_all | solution.py:88
  160.2 172.0 %all-gather.8.cloned.1.call-start = ((), (), s32[]{:S(2)}) async-start(), calls=%async_computation.6 | async-start | bytes 5308416 | tf_op jit(solution)/shard_map/all_gather | solution.py:99
  189.0 29.1 %copy-start.5 = (bf16[24,384]{1,0:T(8,128)(2,1)S(1)}, bf16[24,384]{1,0:T(8,128)(2,1)}, u32[]{:S(2)}) copy-start(bf16[24,384]{1,0:T(8,128)(2,1)} %param.16) | copy-start | bytes 55300
  189.0 29.4 %copy-start.10 = (bf16[384,2,48]{0,2,1:T(8,128)(2,1)S(1)}, bf16[384,2,48]{0,2,1:T(8,128)(2,1)}, u32[]{:S(2)}) copy-start(bf16[384,2,48]{0,2,1:T(8,128)(2,1)} %param.28) | copy-start | bytes 221188
  189.0 29.4 %copy-start.15 = (f32[384]{0:T(512)S(1)}, f32[384]{0:T(512)}, u32[]{:S(2)}) copy-start(f32[384]{0:T(512)} %param.25) | copy-start | bytes 4612
  189.0 29.6 %copy-start.11 = (bf16[384,48]{0,1:T(8,128)(2,1)S(1)}, bf16[384,48]{0,1:T(8,128)(2,1)}, u32[]{:S(2)}) copy-start(bf16[384,48]{0,1:T(8,128)(2,1)} %param.27) | copy-start | bytes 110596
  190.4 67.5 %copy-start.12 = (bf16[384,48]{0,1:T(8,128)(2,1)S(1)}, bf16[384,48]{0,1:T(8,128)(2,1)}, u32[]{:S(2)}) copy-start(bf16[384,48]{0,1:T(8,128)(2,1)} %param.26) | copy-start | bytes 110596
  190.4 67.9 %copy-start.7 = (s32[768]{0:T(1024)S(1)}, s32[768]{0:T(1024)}, u32[]{:S(2)}) copy-start(s32[768]{0:T(1024)} %param.17) | copy-start | bytes 9220
  258.3 78.9 %copy-start.8 = (f32[128]{0:T(128)S(1)}, f32[128]{0:T(128)}, u32[]{:S(2)}) copy-start(f32[128]{0:T(128)} %param.21) | copy-start | bytes 1540
  332.2 3.8 %copy-start.2 = (bf16[128,24,768]{2,1,0:T(8,128)(2,1)S(1)}, bf16[128,24,768]{2,1,0:T(8,128)(2,1)}, u32[]{:S(2)}) copy-start(bf16[128,24,768]{2,1,0:T(8,128)(2,1)} %all-gather.8.cloned.1.call-done) | copy-start | bytes 14155780
  337.2 1.5 copy-start.6
  337.2 2.9 slice-start
  338.7 1.5 slice-start.1
  338.7 1.5 copy-start.14
  345.4 3.7 copy-start.4
  346.9 2.9 copy-start.13
  351.0 13.4 %all-to-all-start.3 = ((bf16[8,2,576]{2,1,0:T(2,128)(2,1)}), bf16[8,2,576]{2,1,0:T(2,128)(2,1)S(1)}, u32[]{:S(2)}, u32[]{:S(2)}) async-start(bf16[8,2,576]{2,1,0:T(2,128)(2,1)} %reshape.173), calls=%async_computation.3 | async-start | bytes 40960 | tf_op jit(solution)/shard_map/all_to_all | solution.py:33
  (1 other events, 1.4 us)
Sparse Core Ops, SparseCore 0:
  10.4 47.7 all-gather.3
  60.0 51.2 all-gather.5
  218.2 113.9 all-gather.7
where the time goes:
time: 372 us
  waiting for transfers between devices  228 us (61%)
  blocking collectives  60.5 us (16%)
  other arithmetic  21.5 us (6%)
  starting transfers between devices  17.9 us (5%)
  local copies, waits for them, and re-layouts  17 us (5%)
  between operations  14.2 us (4%)
  matrix products  12.9 us (3%)
    all_gather x2, waiting for transfers between devices, gathered_by_axis(): shard = lax.all_gather(shard, axis, axis=dim, tiled=True)  101 us
    all_gather x1, waiting for transfers between devices, body(): crossed = lax.all_gather(summed, CHAN, axis=0, tiled=True)  73.8 us
    all_gather x1, blocking collectives, sent_together(): whole = lax.all_gather(both, axis, axis=dim, tiled=True)  38.8 us
    all_to_all x1, waiting for transfers between devices, body(): lax.all_to_all(right_send, 'row', split_axis=0, concat_axis=1, tiled=True)  27.7 us
    all_to_all x1, blocking collectives, body(): lax.all_to_all(owned, 'row', split_axis=1, concat_axis=0, tiled=True)  21.7 us
    all_to_all x1, waiting for transfers between devices, body(): lax.all_to_all(left_send, 'row', split_axis=0, concat_axis=1, tiled=True)  17.5 us
    unnamed x47, local copies, waits for them, and re-layouts  9.37 us
    all_to_all x1, waiting for transfers between devices, sent_and_summed(): lax.all_to_all(cut_along(shard, dim, peers), axis, 0, 0, tiled=True)  7.95 us
  transfers between devices with their start and end apart: 6, of which 6 were waited for; matrix products, arithmetic and copies ran while one was open for 2% of the time, Pallas kernels for 0%

commit v1 on v0

--- a/solution.py
+++ b/solution.py
@@ -96,7 +96,12 @@
         .transpose(0, 2, 1, 3, 4)
         .reshape(chans, rows, width)
     )
-    crossed = lax.all_gather(summed, CHAN, axis=0, tiled=True)
+    crossed = jnp.concatenate(
+        jax.lax.all_to_all(
+            jnp.stack(tuple((summed for _ in range(jax.lax.axis_size(CHAN)))), axis=0), CHAN, 0, 0
+        ),
+        0,
+    )
     product_normed = layer_norm(crossed.astype(jnp.float32), x_gain[:, None, None], 0).astype(
         jnp.bfloat16
     )

time: 372 us -> 420 us (1.13); the launches traced: 372 us -> 413 us
  blocking collectives: 60.5 us -> 155 us
  waiting for transfers between devices: 228 us -> 154 us
  starting transfers between devices: 17.9 us -> 28.7 us
  other arithmetic: 21.5 us -> 28.4 us
    all_gather x1, blocking collectives: 38.8 us -> 133 us  [sent_together(): whole = lax.all_gather(both, axis, axis=dim, tiled=True)]
    all_gather x1 -> x0, waiting for transfers between devices: 73.8 us -> none  [body(): crossed = lax.all_gather(summed, CHAN, axis=0, tiled=True)]
    all_to_all x0 -> x1, starting transfers between devices: none -> 6.03 us  [body(): jax.lax.all_to_all(jnp.stack(tuple((summed for _ in range(jax.lax.axis_si...]
    all_to_all x1, starting transfers between devices: 3.31 us -> 8.22 us  [sent_and_summed(): lax.all_to_all(cut_along(shard, dim, peers), axis, 0, 0, tiled=True)]
  transfers between devices with their start and end apart: 6 -> 6, of which waited for: 6 -> 5; matrix products, arithmetic and copies ran while one was open for 2% -> 2% of each run, Pallas kernels for 0% -> 0%
where the time goes in v1:
time: 420 us; the launch traced here: 413 us
  blocking collectives  155 us (37%)
  waiting for transfers between devices  154 us (37%)
  starting transfers between devices  28.7 us (7%)
  other arithmetic  28.4 us (7%)
  local copies, waits for them, and re-layouts  19 us (5%)
  between operations  14.5 us (3%)
  matrix products  13.4 us (3%)
    all_gather x1, blocking collectives, sent_together(): whole = lax.all_gather(both, axis, axis=dim, tiled=True)  133 us
    all_gather x2, waiting for transfers between devices, gathered_by_axis(): shard = lax.all_gather(shard, axis, axis=dim, tiled=True)  101 us
    all_to_all x1, waiting for transfers between devices, body(): lax.all_to_all(right_send, 'row', split_axis=0, concat_axis=1, tiled=True)  28 us
    all_to_all x1, blocking collectives, body(): lax.all_to_all(owned, 'row', split_axis=1, concat_axis=0, tiled=True)  21.7 us
    all_to_all x1, waiting for transfers between devices, body(): lax.all_to_all(left_send, 'row', split_axis=0, concat_axis=1, tiled=True)  17.6 us
    unnamed x47, local copies, waits for them, and re-layouts  8.73 us
  transfers between devices with their start and end apart: 6, of which 5 were waited for; matrix products, arithmetic and copies ran while one was open for 2% of the time, Pallas kernels for 0%

profile of v1, /device:TPU:2, one launch (start us, length us, event | category | flops | bytes accessed | tf_op | source)
XLA Modules:
  0.0 413.1 jit_solution(843195158555995870)
XLA Ops:
  7.2 2.0 copy.57
  9.3 48.9 %all-gather.3.cloned.1.call-done = bf16[32,24,768]{2,0,1:T(8,128)(2,1)} async-done(((bf16[16,24,768]{2,0,1:T(8,128)(2,1)}), bf16[32,24,768]{2,0,1:T(8,128)(2,1)}) %all-gather.3.cloned.1.call-update) | async-done | bytes 1179664 | tf_op jit(solution)/shard_map/all_gather | solution.py:15
  59.6 51.7 %all-gather.5.cloned.1.call-done = bf16[128,24,768]{2,0,1:T(8,128)(2,1)} async-done(((bf16[32,24,768]{2,0,1:T(8,128)(2,1)}), bf16[128,24,768]{2,0,1:T(8,128)(2,1)}) %all-gather.5.cloned.1.call-update) | async-done | bytes 4718608 | tf_op jit(solution)/shard_map/all_gather | solution.py:15
  111.3 3.2 convert_reduce_fusion
  116.4 1.9 fusion.15
  118.4 2.2 copy-done.3
  120.9 1.7 copy.60
  125.0 7.9 %all-to-all-start = ((bf16[32,12,768]{2,1,0:T(8,128)(2,1)}), bf16[32,12,768]{2,1,0:T(8,128)(2,1)S(1)}, u32[]{:S(2)}, u32[]{:S(2)}) async-start(bf16[32,12,768]{2,1,0:T(8,128)(2,1)} %multiply_convert_fusion), calls=%async_computation | async-start | bytes 1572864 | tf_op jit(solution)/shard_map/all_to_all | solution.py:87
  133.0 2.0 fusion.25
  135.1 17.6 %all-to-all-done = bf16[32,12,768]{2,1,0:T(8,128)(2,1)S(1)} async-done(((bf16[32,12,768]{2,1,0:T(8,128)(2,1)}), bf16[32,12,768]{2,1,0:T(8,128)(2,1)S(1)}, u32[]{:S(2)}, u32[]{:S(2)}) %all-to-all-start) | async-done | bytes 589856 | tf_op jit(solution)/shard_map/all_to_all | solution.py:87
  153.8 6.4 %all-to-all-start.1 = ((bf16[32,24,768]{2,1,0:T(8,128)(2,1)}), bf16[32,24,768]{2,1,0:T(8,128)(2,1)S(1)}, u32[]{:S(2)}, u32[]{:S(2)}) async-start(bf16[32,24,768]{2,1,0:T(8,128)(2,1)} %bitcast.5), calls=%async_computation.1 | async-start | bytes 2359296 | tf_op jit(solution)/shard_map/all_to_all | solution.py:88
  160.4 28.0 %all-to-all-done.1 = bf16[32,24,768]{2,1,0:T(8,128)(2,1)S(1)} async-done(((bf16[32,24,768]{2,1,0:T(8,128)(2,1)}), bf16[32,24,768]{2,1,0:T(8,128)(2,1)S(1)}, u32[]{:S(2)}, u32[]{:S(2)}) %all-to-all-start.1) | async-done | bytes 1179680 | tf_op jit(solution)/shard_map/all_to_all | solution.py:88
  190.4 4.2 %reduce.3 = bf16[384,768]{1,0:T(8,128)(2,1)S(1)} reduce(bf16[384,1,768]{2,1,0:T(2,128)(2,1)S(1)} %bitcast.72, bf16[]{:T(256)} %broadcast.174), dimensions={1}, to_apply=%bitcast.69.reduce_sub_computation | reduce | bytes 1179650
  194.9 21.7 %all_to_all.37 = bf16[32,2,4608]{2,1,0:T(2,128)(2,1)S(1)} all-to-all(bf16[32,2,4608]{2,1,0:T(2,128)(2,1)S(1)} %reshape.177), channel_id=1, replica_groups=mesh['row'=32,'chan_0'=4,'chan_1'=2] {'row'}, dimensions={0} | all-to-all | bytes 1179648 | tf_op jit(solution)/shard_map/all_to_all | solution.py:93
  217.3 2.6 stack.3
  220.0 6.0 %all-to-all-start.3 = ((bf16[8,16,24,768]{3,1,2,0:T(8,128)(2,1)}), bf16[8,16,24,768]{3,1,2,0:T(8,128)(2,1)}, u32[]{:S(2)}, u32[]{:S(2)}) async-start(bf16[8,16,24,768]{3,1,2,0:T(8,128)(2,1)} %stack.3), calls=%async_computation.3 | async-start | bytes 9437184 | tf_op jit(solution)/shard_map/all_to_all | solution.py:100
  226.8 133.1 %all_gather.11 = bf16[768,96]{1,0:T(8,128)(2,1)S(1)} all-gather(bf16[24,96]{1,0:T(8,128)(2,1)S(1)} %pad_maximum_fusion), channel_id=1, replica_groups=mesh['row'=32,'chan_0'=4,'chan_1'=2] {'row'}, dimensions={0}, use_global_device_ids=true | all-gather | bytes 152064 | tf_op jit(solution)/shard_map/all_gather | solution.py:22
  360.6 3.7 fusion.21
  364.3 4.1 multiply_reduce_fusion
  368.5 3.9 copy_convert_fusion
  375.8 5.6 %convert_reduce_fusion.1 = (f32[24,768]{1,0:T(8,128)S(1)}, bf16[128,24,768]{2,0,1:T(8,128)(2,1)S(1)}) fusion(f32[24,768,128]{1,2,0:T(8,128)S(1)} %fusion.17, bf16[128,128]{1,0:T(8,128)(2,1)S(1)} %copy-done.14, bf16[128,24,768]{2,0,1:T(8,128)(2,1)S(1)} %bitcast.71, f32[128]{0:T(128)S(1)} %copy-done.9, f32[24,768]{1,0:T(8,128)S(1)} %add_rsqrt_fusion.2, ...), kind=kOutput, calls=%fused_computation.5 | convolution fusion | flops 636991488 | bytes 19128832 | tf_op jit(solution)/shard_map/cij,cd->dij/dot_general | solution.py:109
  382.9 2.4 fusion.19
  387.1 8.2 %all-to-all-start.4 = ((bf16[8,2,576]{2,1,0:T(2,128)(2,1)}), bf16[8,2,576]{2,1,0:T(2,128)(2,1)S(1)}, u32[]{:S(2)}, u32[]{:S(2)}) async-start(bf16[8,2,576]{2,1,0:T(2,128)(2,1)} %reshape.179), calls=%async_computation.4 | async-start | bytes 40960 | tf_op jit(solution)/shard_map/all_to_all | solution.py:33
  397.5 8.0 %all-to-all-done.4 = bf16[8,2,576]{2,1,0:T(2,128)(2,1)S(1)} async-done(((bf16[8,2,576]{2,1,0:T(2,128)(2,1)}), bf16[8,2,576]{2,1,0:T(2,128)(2,1)S(1)}, u32[]{:S(2)}, u32[]{:S(2)}) %all-to-all-start.4) | async-done | bytes 18464 | tf_op jit(solution)/shard_map/all_to_all | solution.py:33
  (98 shorter events, 21.4 us)
Async XLA Ops:
  7.2 51.1 %copy-start = (bf16[128,4,128]{2,1,0:T(4,128)(2,1)S(1)}, bf16[128,4,128]{2,1,0:T(4,128)(2,1)}, u32[]{:S(2)}) copy-start(bf16[128,4,128]{2,1,0:T(4,128)(2,1)} %param.19) | copy-start | bytes 393220
  7.2 51.0 %all-gather.3.cloned.1.call-start = ((), (), s32[]{:S(2)}) async-start(), calls=%async_computation.5 | async-start | bytes 1769472 | tf_op jit(solution)/shard_map/all_gather | solution.py:15
  9.3 102.0 %all-gather.5.cloned.1.call-start = ((), (), s32[]{:S(2)}) async-start(), calls=%async_computation.6 | async-start | bytes 5898240 | tf_op jit(solution)/shard_map/all_gather | solution.py:15
  59.5 56.9 %copy-start.9 = (f32[128]{0:T(128)S(1)}, f32[128]{0:T(128)}, u32[]{:S(2)}) copy-start(f32[128]{0:T(128)} %param.18) | copy-start | bytes 1540
  111.3 3.8 copy-start.2
  118.4 2.2 copy-start.3
  125.0 27.6 %all-to-all-start = ((bf16[32,12,768]{2,1,0:T(8,128)(2,1)}), bf16[32,12,768]{2,1,0:T(8,128)(2,1)S(1)}, u32[]{:S(2)}, u32[]{:S(2)}) async-start(bf16[32,12,768]{2,1,0:T(8,128)(2,1)} %multiply_convert_fusion), calls=%async_computation | async-start | bytes 1572864 | tf_op jit(solution)/shard_map/all_to_all | solution.py:87
  153.8 34.5 %all-to-all-start.1 = ((bf16[32,24,768]{2,1,0:T(8,128)(2,1)}), bf16[32,24,768]{2,1,0:T(8,128)(2,1)S(1)}, u32[]{:S(2)}, u32[]{:S(2)}) async-start(bf16[32,24,768]{2,1,0:T(8,128)(2,1)} %bitcast.5), calls=%async_computation.1 | async-start | bytes 2359296 | tf_op jit(solution)/shard_map/all_to_all | solution.py:88
  219.9 6.1 %copy-start.5 = (bf16[24,384]{1,0:T(8,128)(2,1)S(1)}, bf16[24,384]{1,0:T(8,128)(2,1)}, u32[]{:S(2)}) copy-start(bf16[24,384]{1,0:T(8,128)(2,1)} %param.16) | copy-start | bytes 55300
  219.9 6.4 %copy-start.10 = (bf16[384,2,48]{0,2,1:T(8,128)(2,1)S(1)}, bf16[384,2,48]{0,2,1:T(8,128)(2,1)}, u32[]{:S(2)}) copy-start(bf16[384,2,48]{0,2,1:T(8,128)(2,1)} %param.28) | copy-start | bytes 221188
  219.9 6.4 %copy-start.15 = (f32[384]{0:T(512)S(1)}, f32[384]{0:T(512)}, u32[]{:S(2)}) copy-start(f32[384]{0:T(512)} %param.25) | copy-start | bytes 4612
  219.9 6.6 %copy-start.11 = (bf16[384,48]{0,1:T(8,128)(2,1)S(1)}, bf16[384,48]{0,1:T(8,128)(2,1)}, u32[]{:S(2)}) copy-start(bf16[384,48]{0,1:T(8,128)(2,1)} %param.27) | copy-start | bytes 110596
  219.9 140.2 %copy-start.12 = (bf16[384,48]{0,1:T(8,128)(2,1)S(1)}, bf16[384,48]{0,1:T(8,128)(2,1)}, u32[]{:S(2)}) copy-start(bf16[384,48]{0,1:T(8,128)(2,1)} %param.26) | copy-start | bytes 110596
  220.0 140.6 %copy-start.7 = (s32[768]{0:T(1024)S(1)}, s32[768]{0:T(1024)}, u32[]{:S(2)}) copy-start(s32[768]{0:T(1024)} %param.17) | copy-start | bytes 9220
  220.0 140.6 %all-to-all-start.3 = ((bf16[8,16,24,768]{3,1,2,0:T(8,128)(2,1)}), bf16[8,16,24,768]{3,1,2,0:T(8,128)(2,1)}, u32[]{:S(2)}, u32[]{:S(2)}) async-start(bf16[8,16,24,768]{3,1,2,0:T(8,128)(2,1)} %stack.3), calls=%async_computation.3 | async-start | bytes 9437184 | tf_op jit(solution)/shard_map/all_to_all | solution.py:100
  368.4 3.9 copy-start.8
  372.3 2.7 slice-start
  373.6 2.2 slice-start.1
  373.6 2.2 copy-start.14
  381.4 3.9 copy-start.4
  381.4 1.4 copy-start.16
  382.8 23.4 %copy-start.1 = (bf16[128,4,128]{2,1,0:T(4,128)(2,1)S(1)}, bf16[128,4,128]{2,1,0:T(4,128)(2,1)}, u32[]{:S(2)}) copy-start(bf16[128,4,128]{2,1,0:T(4,128)(2,1)} %param.19) | copy-start | bytes 393220
  382.9 3.1 copy-start.13
  387.1 18.4 %all-to-all-start.4 = ((bf16[8,2,576]{2,1,0:T(2,128)(2,1)}), bf16[8,2,576]{2,1,0:T(2,128)(2,1)S(1)}, u32[]{:S(2)}, u32[]{:S(2)}) async-start(bf16[8,2,576]{2,1,0:T(2,128)(2,1)} %reshape.179), calls=%async_computation.4 | async-start | bytes 40960 | tf_op jit(solution)/shard_map/all_to_all | solution.py:33
  (1 other events, 1.2 us)
Sparse Core Ops, SparseCore 0:
  10.4 47.7 all-gather.2
  60.0 51.2 all-gather.4
